TPU v7x, 128 devices: a whole 4x4x4 slice. The times are simulated.
128 devices in a mesh: src: 16 (over z, x), rcv: 8 (over y, core).
Axes of the slice: x: 4, y: 4, z: 4, core: 2. Of those that a mesh axis runs over, the one named last changes fastest.
Arguments:
- traces: bfloat16 [2, 2, 2048, 2048], P(None, None, 'src', 'rcv'), may hold values from -8 to 8
- wavelet: float32 [2, 2], replicated, may hold values from -0.3 to 0.3
Outputs:
- coeffs: float32 [2, 2, 2048, 2048], P(None, None, 'src', 'rcv')
- norms: float32 [2, 2], replicated
All inputs are finite; a program needn't handle non-finite values.
Results may differ from a plain program's by a relative error of at most 0.006.
Values may be sent and summed in bfloat16 or wider, within the bound.
A program may use at most 128 MiB of HBM per device.

v0:
```python
import math
import jax
import jax.numpy as jnp
from jax import lax
from jax.sharding import Mesh
from jax.sharding import PartitionSpec as P

ITERS = 2
SRC = ("src_0", "src_1")
RCV = ("rcv_0", "rcv_1")
SRC_RCV = ("src_0", "src_1", "rcv_0", "rcv_1")
step_length = 0.4
shrink_fraction = 0.2


def laid_out(tiles, dim):
    shape = list(tiles.shape[1:])
    shape[dim] *= tiles.shape[0]
    return jnp.moveaxis(tiles, 0, dim).reshape(shape)


def copy_for_each(x, axis):
    copies = jnp.broadcast_to(x, (lax.axis_size(axis), *x.shape))
    return lax.all_to_all(copies, axis, split_axis=0, concat_axis=0, tiled=True)


def gathered_copies(x, axis, dim):
    return laid_out(copy_for_each(x, axis), dim)


def all_in_one(x, axis):
    leaves = jax.tree.leaves(x)
    order = sorted(range(len(leaves)), key=lambda k: -leaves[k].size)
    width = (1, *leaves[order[0]].shape)[-1]
    lines = [
        jnp.pad(leaves[k].reshape(-1), (0, -leaves[k].size % width)).reshape(-1, width)
        for k in order
    ]
    both, at, found = (lax.all_gather(jnp.concatenate(lines), axis), 0, {})
    for k, line in zip(order, lines):
        share = both[:, at : at + len(line)].reshape(len(both), -1)
        found[k] = share[:, : leaves[k].size].reshape(-1, *leaves[k].shape)
        at += len(line)
    numbers = iter(range(len(leaves)))
    return jax.tree.map(lambda _: found[next(numbers)], x)


def once_a_type(x, axis):
    leaves, found = (jax.tree.leaves(x), {})
    for first, a in enumerate(leaves):
        if first not in found:
            alike = [k for k, b in enumerate(leaves) if b.dtype == a.dtype]
            got = (
                all_in_one([leaves[k] for k in alike], axis)
                if len(alike) > 1
                else [lax.all_gather(a, axis)]
            )
            for k, b in zip(alike, got):
                found[k] = b
    numbers = iter(range(len(leaves)))
    return jax.tree.map(lambda _: found[next(numbers)], x)


def joined_all(x, axes, combine):
    for axis in axes:
        pieces = once_a_type(x, axis)
        x = jax.tree.map(lambda part: part[0], pieces)
        for k in range(1, lax.axis_size(axis)):
            x = combine(x, jax.tree.map(lambda part: part[k], pieces))
    return x


def table_block(offset, height, second, breadth, length, direction):
    left_index = offset + jnp.arange(height, dtype=jnp.int32)
    right_index = second + jnp.arange(breadth, dtype=jnp.int32)
    phase = left_index[:, None] * right_index[None, :] % length
    angle = phase.astype(jnp.float32) * (2.0 * math.pi / length)
    scale = 1.0 / math.sqrt(length)
    return jnp.stack([jnp.cos(angle) * scale, direction * (jnp.sin(angle) * scale)]).astype(
        jnp.bfloat16
    )


def complex_product(left_side, right_side, pattern, left_table, right_table):
    left_re = left_side[0] if left_table else left_side[:, 0]
    left_im = left_side[1] if left_table else left_side[:, 1]
    right_re = right_side[0] if right_table else right_side[:, 0]
    right_im = right_side[1] if right_table else right_side[:, 1]

    def single(first_op, second_op):
        return jnp.einsum(pattern, first_op, second_op, preferred_element_type=jnp.float32)

    real_part = single(left_re, right_re) - single(left_im, right_im)
    imag_part = single(left_re, right_im) + single(left_im, right_re)
    return jnp.stack([real_part, imag_part], axis=1)


def complex_scale(real_part, imag_part, values):
    return jnp.stack(
        [
            real_part * values[:, 0] - imag_part * values[:, 1],
            real_part * values[:, 1] + imag_part * values[:, 0],
        ],
        axis=1,
    )


def combine_stats(first_pair, second_pair):
    return (jnp.maximum(first_pair[0], second_pair[0]), first_pair[1] + second_pair[1])


def per_device(traces, wavelet):
    row_count = traces.shape[2]
    col_count = traces.shape[3]
    extent = row_count * lax.axis_size(SRC)
    row_anchor = lax.axis_index(SRC) * row_count
    col_anchor = lax.axis_index(RCV) * col_count
    root_scale = 1.0 / math.sqrt(extent)
    wave_re = (wavelet[:, 0] * root_scale)[:, None, None]
    wave_im = (wavelet[:, 1] * root_scale)[:, None, None]
    forward_cols = table_block(0, extent, col_anchor, col_count, extent, -1.0)
    forward_rows = table_block(row_anchor, row_count, 0, extent, extent, -1.0)
    inverse_cols = table_block(0, extent, col_anchor, col_count, extent, 1.0)
    inverse_rows = table_block(row_anchor, row_count, 0, extent, extent, 1.0)
    coeffs = jnp.zeros(traces.shape, jnp.float32)
    columns_all = lax.all_gather(traces, SRC, axis=2, tiled=True)
    traces_f = traces.astype(jnp.float32)

    def column_section(table, portion):
        return complex_product(table, portion, "mn,fnc->fmc", True, False)

    def paired(first_op, second_op):
        return jnp.einsum("fmr,fkr->fmk", first_op, second_op, preferred_element_type=jnp.float32)

    norm_list = []
    for iteration in range(ITERS):
        if iteration == 0:
            misfit = traces_f
        else:
            coeff_half = coeffs.astype(jnp.bfloat16)
            halfway = column_section(
                inverse_rows, lax.all_gather(coeff_half, SRC, axis=2, tiled=True)
            ).astype(jnp.bfloat16)
            model = complex_product(
                gathered_copies(halfway, RCV, 3), inverse_cols, "fmn,nc->fmc", False, True
            ).astype(jnp.bfloat16)
            product = complex_product(
                gathered_copies(model, RCV, 3), columns_all, "fmn,fnc->fmc", False, False
            )
            misfit = traces_f - model.astype(jnp.float32) + complex_scale(wave_re, wave_im, product)
        local_squares = jnp.sum(misfit * misfit, axis=(1, 2, 3))
        misfit_half = misfit.astype(jnp.bfloat16)
        misfit_re = misfit_half[:, 0]
        misfit_im = misfit_half[:, 1]
        column_re = columns_all[:, 0]
        column_im = columns_all[:, 1]
        back_re = paired(misfit_re, column_re) + paired(misfit_im, column_re * 0 + column_im)
        back_im = paired(misfit_im, column_re) - paired(misfit_re, column_im)
        scaled = complex_scale(wave_re, -wave_im, jnp.stack([back_re, back_im], axis=1))
        embedded = lax.dynamic_update_slice(
            jnp.zeros_like(scaled), misfit_half.astype(jnp.float32), (0, 0, 0, col_anchor)
        )
        gradient_rows = lax.psum(embedded - scaled, RCV)
        halfway = complex_product(
            gradient_rows.astype(jnp.bfloat16), forward_cols, "fmn,nc->fmc", False, True
        ).astype(jnp.bfloat16)
        spectrum = column_section(forward_rows, lax.all_gather(halfway, SRC, axis=2, tiled=True))
        trial = coeffs + step_length * spectrum
        magnitude = jnp.sqrt(trial[:, 0] * trial[:, 0] + trial[:, 1] * trial[:, 1])
        local_peak = jnp.max(magnitude, axis=(1, 2))
        global_peak, total_squares = joined_all((local_peak, local_squares), SRC_RCV, combine_stats)
        norm_list.append(jnp.sqrt(total_squares))
        level = shrink_fraction * global_peak[:, None, None]
        factor = jnp.maximum(1.0 - level / jnp.maximum(magnitude, level), 0.0)
        coeffs = trial * factor[:, None]
    return (coeffs, jnp.stack(norm_list))


def solution(mesh):
    split = Mesh(mesh.devices.reshape(4, 4, 4, 2), ("src_0", "src_1", "rcv_0", "rcv_1"))
    return jax.shard_map(
        per_device,
        mesh=split,
        in_specs=(P(None, None, SRC, RCV), P()),
        out_specs=(P(None, None, SRC, RCV), P()),
        check_vma=False,
    )
```

profile of v0, /device:TPU:1, one launch (start us, length us, event | category | flops | bytes accessed | tf_op | source)
XLA Modules:
  0.0 641.2 jit_solution(3735553232752024656)
XLA Ops:
  13.3 51.9 %all-gather.21.cloned.1.call-done = bf16[2,2,2048,256]{3,2,0,1:T(8,128)(2,1)} async-done(((bf16[2,2,128,256]{3,2,0,1:T(8,128)(2,1)}), bf16[2,2,2048,256]{3,2,0,1:T(8,128)(2,1)}) %all-gather.21.cloned.1.call-update) | async-done | bytes 4194320 | tf_op jit(solution)/shard_map/all_gather | solution.py:126
  75.7 56.5 %all-reduce.2 = bf16[2,2,128,2048]{3,2,0,1:T(8,128)(2,1)S(1)} all-reduce(f32[2,2,128,2048]{3,2,0,1:T(8,128)} %maximum_subtract_fusion), channel_id=1, replica_groups=mesh['src_0'=4,'src_1'=4,'rcv_0'=4,'rcv_1'=2] {'rcv_0','rcv_1'}, use_global_device_ids=true, to_apply=%region_0.1 | all-reduce | flops 1048576 | bytes 6291456 | tf_op jit(solution)/shard_map/psum | solution.py:163
  132.2 7.9 %fusion.62 = f32[2,128,256]{2,1,0:T(8,128)S(1)} fusion(s32[256]{0:T(256)S(1)} %iota_add_fusion, bf16[2,2,128,2048]{3,2,0,1:T(8,128)(2,1)S(1)} %all-reduce.2), kind=kOutput, calls=%fused_computation.104 | convolution fusion | flops 276824064 | bytes 1311744 | tf_op jit(solution)/shard_map/fmn,nc->fmc/dot_general | solution.py:91
  140.1 8.1 %fusion.67 = f32[2,128,256]{2,1,0:T(8,128)S(1)} fusion(s32[256]{0:T(256)S(1)} %iota_add_fusion, bf16[2,2,128,2048]{3,2,0,1:T(8,128)(2,1)S(1)} %all-reduce.2), kind=kOutput, calls=%fused_computation.106 | convolution fusion | flops 276824064 | bytes 1311744 | tf_op jit(solution)/shard_map/fmn,nc->fmc/dot_general | solution.py:91
  148.3 8.2 %fusion.44 = bf16[2,1,128,256]{3,2,0,1:T(8,128)(2,1)S(1)} fusion(f32[2,128,256]{2,1,0:T(8,128)S(1)} %fusion.62, s32[256]{0:T(256)S(1)} %iota_add_fusion, bf16[2,2,128,2048]{3,2,0,1:T(8,128)(2,1)S(1)} %all-reduce.2), kind=kOutput, calls=%fused_computation.80 | convolution fusion | flops 276955136 | bytes 1442816 | tf_op jit(solution)/shard_map/fmn,nc->fmc/dot_general | solution.py:91
  156.4 7.9 %fusion.43 = bf16[2,1,128,256]{3,2,0,1:T(8,128)(2,1)S(1)} fusion(f32[2,128,256]{2,1,0:T(8,128)S(1)} %fusion.67, s32[256]{0:T(256)S(1)} %iota_add_fusion, bf16[2,2,128,2048]{3,2,0,1:T(8,128)(2,1)S(1)} %all-reduce.2), kind=kOutput, calls=%fused_computation.79 | convolution fusion | flops 276955136 | bytes 1442816 | tf_op jit(solution)/shard_map/fmn,nc->fmc/dot_general | solution.py:91
  165.5 51.1 %all-gather.23.cloned.1.call-done = bf16[2,2,2048,256]{3,2,0,1:T(8,128)(2,1)} async-done(((bf16[2,2,128,256]{3,2,0,1:T(8,128)(2,1)}), bf16[2,2,2048,256]{3,2,0,1:T(8,128)(2,1)}) %all-gather.23.cloned.1.call-update) | async-done | bytes 4194320 | tf_op jit(solution)/shard_map/all_gather | solution.py:167
  249.6 7.8 %all-gather.10 = f32[4,2,2]{2,1,0:T(2,128)S(1)} all-gather(f32[1,2,2]{2,1,0:T(2,128)S(1)} %maximum_bitcast_fusion.3), channel_id=4, replica_groups=mesh['src_0'=4,'src_1'=4,'rcv_0'=4,'rcv_1'=2] {'rcv_0'}, dimensions={0}, use_global_device_ids=true | all-gather | bytes 80 | tf_op jit(solution)/shard_map/all_gather | solution.py:39
  257.4 8.2 %all-gather.11 = f32[2,2,2]{2,1,0:T(2,128)S(1)} all-gather(f32[1,2,2]{2,1,0:T(2,128)S(1)} %maximum_bitcast_fusion.4), channel_id=5, replica_groups=mesh['src_0'=4,'src_1'=4,'rcv_0'=4,'rcv_1'=2] {'rcv_1'}, dimensions={0}, use_global_device_ids=true | all-gather | bytes 48 | tf_op jit(solution)/shard_map/all_gather | solution.py:39
  267.0 50.0 %all-gather.25.cloned.1.call-done = bf16[2,2,2048,256]{2,3,0,1:T(8,128)(2,1)} async-done(((bf16[2,2,128,256]{2,3,0,1:T(8,128)(2,1)}), bf16[2,2,2048,256]{2,3,0,1:T(8,128)(2,1)}) %all-gather.25.cloned.1.call-update) | async-done | bytes 4194320 | tf_op jit(solution)/shard_map/all_gather | solution.py:142
  336.9 32.3 %all_to_all.10 = bf16[8,2,2,128,256]{4,3,1,2,0:T(8,128)(2,1)S(1)} all-to-all(bf16[8,2,2,128,256]{4,3,1,2,0:T(8,128)(2,1)S(1)} %broadcast_in_dim.4), channel_id=1, replica_groups=mesh['src_0'=4,'src_1'=4,'rcv_0'=4,'rcv_1'=2] {'rcv_0','rcv_1'}, dimensions={0} | all-to-all | bytes 4194304 | tf_op jit(solution)/shard_map/all_to_all | solution.py:24
  369.5 7.9 %fusion.59 = f32[2,128,256]{2,1,0:T(8,128)S(1)} fusion(s32[256]{0:T(256)S(1)} %iota_add_fusion, bf16[2,2,128,2048]{3,2,0,1:T(8,128)(2,1)S(1)} %bitcast.296), kind=kOutput, calls=%fused_computation.103 | convolution fusion | flops 276824064 | bytes 1311744 | tf_op jit(solution)/shard_map/fmn,nc->fmc/dot_general | solution.py:91
  377.4 8.3 %fusion.70 = f32[2,128,256]{2,1,0:T(8,128)S(1)} fusion(s32[256]{0:T(256)S(1)} %iota_add_fusion, bf16[2,2,128,2048]{3,2,0,1:T(8,128)(2,1)S(1)} %bitcast.297), kind=kOutput, calls=%fused_computation.107 | convolution fusion | flops 276824064 | bytes 1311744 | tf_op jit(solution)/shard_map/fmn,nc->fmc/dot_general | solution.py:91
  385.7 8.1 %fusion.42 = bf16[2,1,128,256]{3,2,0,1:T(8,128)(2,1)S(1)} fusion(f32[2,128,256]{2,1,0:T(8,128)S(1)} %fusion.59, s32[256]{0:T(256)S(1)} %iota_add_fusion, bf16[2,2,128,2048]{3,2,0,1:T(8,128)(2,1)S(1)} %bitcast.298), kind=kOutput, calls=%fused_computation.78 | convolution fusion | flops 276955136 | bytes 1442816 | tf_op jit(solution)/shard_map/fmn,nc->fmc/dot_general | solution.py:91
  393.9 7.9 %fusion.41 = bf16[2,1,128,256]{3,2,0,1:T(8,128)(2,1)S(1)} fusion(f32[2,128,256]{2,1,0:T(8,128)S(1)} %fusion.70, s32[256]{0:T(256)S(1)} %iota_add_fusion, bf16[2,2,128,2048]{3,2,0,1:T(8,128)(2,1)S(1)} %bitcast.299), kind=kOutput, calls=%fused_computation.77 | convolution fusion | flops 276955136 | bytes 1442816 | tf_op jit(solution)/shard_map/fmn,nc->fmc/dot_general | solution.py:91
  402.0 29.7 %all_to_all.11 = bf16[8,2,2,128,256]{4,3,1,2,0:T(8,128)(2,1)S(1)} all-to-all(bf16[8,2,2,128,256]{4,3,1,2,0:T(8,128)(2,1)S(1)} %broadcast_in_dim.5), channel_id=1, replica_groups=mesh['src_0'=4,'src_1'=4,'rcv_0'=4,'rcv_1'=2] {'rcv_0','rcv_1'}, dimensions={0} | all-to-all | bytes 4194304 | tf_op jit(solution)/shard_map/all_to_all | solution.py:24
  442.6 56.6 %all-reduce.3 = bf16[2,2,128,2048]{3,2,0,1:T(8,128)(2,1)S(1)} all-reduce(f32[2,2,128,2048]{3,2,0,1:T(8,128)} %maximum_subtract_fusion.1), channel_id=1, replica_groups=mesh['src_0'=4,'src_1'=4,'rcv_0'=4,'rcv_1'=2] {'rcv_0','rcv_1'}, use_global_device_ids=true, to_apply=%region_3.4 | all-reduce | flops 1048576 | bytes 6291456 | tf_op jit(solution)/shard_map/psum | solution.py:163
  499.2 7.9 %fusion.56 = f32[2,128,256]{2,1,0:T(8,128)S(1)} fusion(s32[256]{0:T(256)S(1)} %iota_add_fusion, bf16[2,2,128,2048]{3,2,0,1:T(8,128)(2,1)S(1)} %all-reduce.3), kind=kOutput, calls=%fused_computation.102 | convolution fusion | flops 276824064 | bytes 1311744 | tf_op jit(solution)/shard_map/fmn,nc->fmc/dot_general | solution.py:91
  507.1 8.1 %fusion.64 = f32[2,128,256]{2,1,0:T(8,128)S(1)} fusion(s32[256]{0:T(256)S(1)} %iota_add_fusion, bf16[2,2,128,2048]{3,2,0,1:T(8,128)(2,1)S(1)} %all-reduce.3), kind=kOutput, calls=%fused_computation.105 | convolution fusion | flops 276824064 | bytes 1311744 | tf_op jit(solution)/shard_map/fmn,nc->fmc/dot_general | solution.py:91
  515.2 8.2 %fusion.40 = bf16[2,1,128,256]{3,2,0,1:T(8,128)(2,1)S(1)} fusion(f32[2,128,256]{2,1,0:T(8,128)S(1)} %fusion.56, s32[256]{0:T(256)S(1)} %iota_add_fusion, bf16[2,2,128,2048]{3,2,0,1:T(8,128)(2,1)S(1)} %all-reduce.3), kind=kOutput, calls=%fused_computation.76 | convolution fusion | flops 276955136 | bytes 1442816 | tf_op jit(solution)/shard_map/fmn,nc->fmc/dot_general | solution.py:91
  523.4 7.9 %fusion.39 = bf16[2,1,128,256]{3,2,0,1:T(8,128)(2,1)S(1)} fusion(f32[2,128,256]{2,1,0:T(8,128)S(1)} %fusion.64, s32[256]{0:T(256)S(1)} %iota_add_fusion, bf16[2,2,128,2048]{3,2,0,1:T(8,128)(2,1)S(1)} %all-reduce.3), kind=kOutput, calls=%fused_computation.75 | convolution fusion | flops 276955136 | bytes 1442816 | tf_op jit(solution)/shard_map/fmn,nc->fmc/dot_general | solution.py:91
  532.0 51.3 %all-gather.27.cloned.1.call-done = bf16[2,2,2048,256]{3,2,0,1:T(8,128)(2,1)} async-done(((bf16[2,2,128,256]{3,2,0,1:T(8,128)(2,1)}), bf16[2,2,2048,256]{3,2,0,1:T(8,128)(2,1)}) %all-gather.27.cloned.1.call-update) | async-done | bytes 4194320 | tf_op jit(solution)/shard_map/all_gather | solution.py:167
  616.7 7.8 %all-gather.14 = f32[4,2,2]{2,1,0:T(2,128)S(1)} all-gather(f32[1,2,2]{2,1,0:T(2,128)S(1)} %maximum_bitcast_fusion.7), channel_id=8, replica_groups=mesh['src_0'=4,'src_1'=4,'rcv_0'=4,'rcv_1'=2] {'rcv_0'}, dimensions={0}, use_global_device_ids=true | all-gather | bytes 80 | tf_op jit(solution)/shard_map/all_gather | solution.py:39
  624.5 8.2 %all-gather.15 = f32[2,2,2]{2,1,0:T(2,128)S(1)} all-gather(f32[1,2,2]{2,1,0:T(2,128)S(1)} %maximum_bitcast_fusion.8), channel_id=9, replica_groups=mesh['src_0'=4,'src_1'=4,'rcv_0'=4,'rcv_1'=2] {'rcv_1'}, dimensions={0}, use_global_device_ids=true | all-gather | bytes 48 | tf_op jit(solution)/shard_map/all_gather | solution.py:39
  (94 shorter events, 119.3 us)
Async XLA Ops:
  7.2 58.1 %all-gather.21.cloned.1.call-start = ((), (), s32[]{:S(2)}) async-start(), calls=%async_computation.2 | async-start | bytes 4456448 | tf_op jit(solution)/shard_map/all_gather | solution.py:126
  8.9 207.7 %all-gather.23.cloned.1.call-start = ((), (), s32[]{:S(2)}) async-start(), calls=%async_computation.3 | async-start | bytes 4456448 | tf_op jit(solution)/shard_map/all_gather | solution.py:167
  10.0 2.5 copy-start.2
  65.3 2.8 copy-start
  165.1 151.9 %all-gather.25.cloned.1.call-start = ((), (), s32[]{:S(2)}) async-start(), calls=%async_computation.4 | async-start | bytes 4456448 | tf_op jit(solution)/shard_map/all_gather | solution.py:142
  216.7 6.0 copy-start.3
  266.5 316.8 %all-gather.27.cloned.1.call-start = ((), (), s32[]{:S(2)}) async-start(), calls=%async_computation.5 | async-start | bytes 4456448 | tf_op jit(solution)/shard_map/all_gather | solution.py:167
  317.0 6.1 copy-start.4
  431.7 2.2 copy-start.1
  583.3 6.4 %copy-start.5 = (bf16[2,2,2048,256]{3,2,0,1:T(8,128)(2,1)S(1)}, bf16[2,2,2048,256]{3,2,0,1:T(8,128)(2,1)}, u32[]{:S(2)}) copy-start(bf16[2,2,2048,256]{3,2,0,1:T(8,128)(2,1)} %all-gather.27.cloned.1.call-done) | copy-start | bytes 12582916
Sparse Core Ops, SparseCore 0:
  10.7 54.5 all-gather.20
  165.2 51.4 all-gather.22
  266.6 50.2 all-gather.24
  532.2 51.0 all-gather.26
where the time goes:
time: 645 us; the launch traced here: 641 us
  blocking collectives  234 us (36%)
  waiting for transfers between devices  204 us (32%)
  matrix products  165 us (26%)
  between operations  14.4 us (2%)
  other arithmetic  13.8 us (2%)
  local copies, waits for them, and re-layouts  9 us (1%)
    dot_general x28, matrix products, single(): jnp.einsum(pattern, first_op, second_op, preferred_element_type=jnp.float32)  156 us
    psum x2, blocking collectives, per_device(): gradient_rows = lax.psum(embedded - scaled, RCV)  113 us
    all_gather x2, waiting for transfers between devices, per_device(): lax.all_gather(halfway, SRC, axis=2, tiled=True)  102 us
    all_to_all x2, blocking collectives, copy_for_each(): return lax.all_to_all(copies, axis, split_axis=0, concat_axis=0, tiled=True)  61.9 us
    all_gather x8, blocking collectives, all_in_one(): both, at, found = (lax.all_gather(jnp.concatenate(lines), axis), 0, {})  59 us
    all_gather x1, waiting for transfers between devices, per_device(): columns_all = lax.all_gather(traces, SRC, axis=2, tiled=True)  51.9 us
    all_gather x1, waiting for transfers between devices, per_device(): lax.all_gather(coeff_half, SRC, axis=2, tiled=True)  50 us
  transfers between devices with their start and end apart: 4, of which 4 were waited for; matrix products, arithmetic and copies ran while one was open for 1% of the time, Pallas kernels for 0%

commit v1 on v0

--- a/solution.py
+++ b/solution.py
@@ -11,6 +11,11 @@
 SRC_RCV = ("src_0", "src_1", "rcv_0", "rcv_1")
 step_length = 0.4
 shrink_fraction = 0.2
+
+
+def targets_define(block_in):
+    known = lax.all_gather(block_in, RCV).sum(axis=0)
+    return known
 
 
 def laid_out(tiles, dim):
@@ -160,7 +165,7 @@
         embedded = lax.dynamic_update_slice(
             jnp.zeros_like(scaled), misfit_half.astype(jnp.float32), (0, 0, 0, col_anchor)
         )
-        gradient_rows = lax.psum(embedded - scaled, RCV)
+        gradient_rows = targets_define(embedded - scaled)
         halfway = complex_product(
             gradient_rows.astype(jnp.bfloat16), forward_cols, "fmn,nc->fmc", False, True
         ).astype(jnp.bfloat16)

time: 645 us -> 870 us (1.35)
  waiting for transfers between devices: 204 us -> 516 us
  blocking collectives: 234 us -> 121 us
  other arithmetic: 13.8 us -> 39.7 us
    all_gather x0 -> x2, waiting for transfers between devices: none -> 310 us  [targets_define(): known = lax.all_gather(block_in, RCV).sum(axis=0)]
    psum x2 -> x0, blocking collectives: 113 us -> none  [per_device(): gradient_rows = lax.psum(embedded - scaled, RCV)]
    reduce_sum x0 -> x2, other arithmetic: none -> 25.8 us  [targets_define(): known = lax.all_gather(block_in, RCV).sum(axis=0)]
  transfers between devices with their start and end apart: 4 -> 6, of which waited for: 4 -> 6; matrix products, arithmetic and copies ran while one was open for 1% -> 0% of each run, Pallas kernels for 0% -> 0%
where the time goes in v1:
time: 870 us; the launch traced here: 866 us
  waiting for transfers between devices  516 us (59%)
  matrix products  165 us (19%)
  blocking collectives  121 us (14%)
  other arithmetic  39.7 us (5%)
  between operations  14.7 us (2%)
  local copies, waits for them, and re-layouts  8.96 us (1%)
    all_gather x2, waiting for transfers between devices, targets_define(): known = lax.all_gather(block_in, RCV).sum(axis=0)  310 us
    dot_general x28, matrix products, single(): jnp.einsum(pattern, first_op, second_op, preferred_element_type=jnp.float32)  156 us
    all_gather x2, waiting for transfers between devices, per_device(): lax.all_gather(halfway, SRC, axis=2, tiled=True)  104 us
    all_to_all x2, blocking collectives, copy_for_each(): return lax.all_to_all(copies, axis, split_axis=0, concat_axis=0, tiled=True)  61.9 us
    all_gather x8, blocking collectives, all_in_one(): both, at, found = (lax.all_gather(jnp.concatenate(lines), axis), 0, {})  59 us
    all_gather x1, waiting for transfers between devices, per_device(): columns_all = lax.all_gather(traces, SRC, axis=2, tiled=True)  51.9 us
    all_gather x1, waiting for transfers between devices, per_device(): lax.all_gather(coeff_half, SRC, axis=2, tiled=True)  50 us
    reduce_sum x2, other arithmetic, targets_define(): known = lax.all_gather(block_in, RCV).sum(axis=0)  25.8 us
  transfers between devices with their start and end apart: 6, of which 6 were waited for; matrix products, arithmetic and copies ran while one was open for 0% of the time, Pallas kernels for 0%

profile of v1, /device:TPU:1, one launch (start us, length us, event | category | flops | bytes accessed | tf_op | source)
XLA Modules:
  0.0 866.1 jit_solution(16160079391879457118)
XLA Ops:
  13.3 51.9 %all-gather.25.cloned.1.call-done = bf16[2,2,2048,256]{3,2,0,1:T(8,128)(2,1)} async-done(((bf16[2,2,128,256]{3,2,0,1:T(8,128)(2,1)}), bf16[2,2,2048,256]{3,2,0,1:T(8,128)(2,1)}) %all-gather.25.cloned.1.call-update) | async-done | bytes 4194320 | tf_op jit(solution)/shard_map/all_gather | solution.py:131
  75.8 156.1 %all-gather.33.cloned.1.call-done = f32[16,2,128,2048]{3,2,0,1:T(8,128)} async-done(((f32[2,2,128,2048]{3,2,0,1:T(8,128)}), f32[16,2,128,2048]{3,2,0,1:T(8,128)}) %all-gather.33.cloned.1.call-update) | async-done | bytes 33554448 | tf_op jit(solution)/shard_map/all_gather | solution.py:17
  231.9 12.9 %reduce_sum.36 = bf16[2,2,128,2048]{3,2,0,1:T(8,128)(2,1)S(1)} reduce(f32[8,2,2,128,2048]{4,3,1,0,2:T(8,128)} %bitcast.292, f32[]{:T(128)} %constant.28.clone.1), dimensions={0}, to_apply=%region_0.1 | reduce | flops 7340032 | bytes 35651588 | tf_op jit(solution)/shard_map/reduce_sum | solution.py:17
  244.9 7.9 fusion.62
  252.8 8.1 fusion.67
  260.9 8.2 fusion.44
  269.1 7.9 fusion.43
  278.2 51.6 %all-gather.27.cloned.1.call-done = bf16[2,2,2048,256]{3,2,0,1:T(8,128)(2,1)} async-done(((bf16[2,2,128,256]{3,2,0,1:T(8,128)(2,1)}), bf16[2,2,2048,256]{3,2,0,1:T(8,128)(2,1)}) %all-gather.27.cloned.1.call-update) | async-done | bytes 4194320 | tf_op jit(solution)/shard_map/all_gather | solution.py:172
  370.5 8.2 all-gather.13
  380.1 50.0 %all-gather.29.cloned.1.call-done = bf16[2,2,2048,256]{2,3,0,1:T(8,128)(2,1)} async-done(((bf16[2,2,128,256]{2,3,0,1:T(8,128)(2,1)}), bf16[2,2,2048,256]{2,3,0,1:T(8,128)(2,1)}) %all-gather.29.cloned.1.call-update) | async-done | bytes 4194320 | tf_op jit(solution)/shard_map/all_gather | solution.py:147
  450.0 32.3 %all_to_all.10 = bf16[8,2,2,128,256]{4,3,1,2,0:T(8,128)(2,1)S(1)} all-to-all(bf16[8,2,2,128,256]{4,3,1,2,0:T(8,128)(2,1)S(1)} %broadcast_in_dim.4), channel_id=1, replica_groups=mesh['src_0'=4,'src_1'=4,'rcv_0'=4,'rcv_1'=2] {'rcv_0','rcv_1'}, dimensions={0} | all-to-all | bytes 4194304 | tf_op jit(solution)/shard_map/all_to_all | solution.py:29
  482.6 7.9 fusion.59
  490.5 8.3 fusion.70
  498.8 8.1 fusion.42
  507.0 7.9 fusion.41
  515.1 29.7 %all_to_all.11 = bf16[8,2,2,128,256]{4,3,1,2,0:T(8,128)(2,1)S(1)} all-to-all(bf16[8,2,2,128,256]{4,3,1,2,0:T(8,128)(2,1)S(1)} %broadcast_in_dim.5), channel_id=1, replica_groups=mesh['src_0'=4,'src_1'=4,'rcv_0'=4,'rcv_1'=2] {'rcv_0','rcv_1'}, dimensions={0} | all-to-all | bytes 4194304 | tf_op jit(solution)/shard_map/all_to_all | solution.py:29
  556.0 154.2 %all-gather.35.cloned.1.call-done = f32[16,2,128,2048]{3,2,0,1:T(8,128)} async-done(((f32[2,2,128,2048]{3,2,0,1:T(8,128)}), f32[16,2,128,2048]{3,2,0,1:T(8,128)}) %all-gather.35.cloned.1.call-update) | async-done | bytes 33554448 | tf_op jit(solution)/shard_map/all_gather | solution.py:17
  710.1 12.8 %reduce_sum.38 = bf16[2,2,128,2048]{3,2,0,1:T(8,128)(2,1)S(1)} reduce(f32[8,2,2,128,2048]{4,3,1,0,2:T(8,128)} %bitcast.293, f32[]{:T(128)} %constant.28.clone.1), dimensions={0}, to_apply=%region_3.4 | reduce | flops 7340032 | bytes 35651588 | tf_op jit(solution)/shard_map/reduce_sum | solution.py:17
  722.9 7.9 fusion.56
  730.8 8.1 fusion.64
  739.0 8.2 fusion.40
  747.1 7.9 fusion.39
  755.8 52.0 %all-gather.31.cloned.1.call-done = bf16[2,2,2048,256]{3,2,0,1:T(8,128)(2,1)} async-done(((bf16[2,2,128,256]{3,2,0,1:T(8,128)(2,1)}), bf16[2,2,2048,256]{3,2,0,1:T(8,128)(2,1)}) %all-gather.31.cloned.1.call-update) | async-done | bytes 4194320 | tf_op jit(solution)/shard_map/all_gather | solution.py:172
  849.0 8.2 all-gather.17
  (100 shorter events, 135.1 us)
Async XLA Ops:
  7.2 58.1 %all-gather.25.cloned.1.call-start = ((), (), s32[]{:S(2)}) async-start(), calls=%async_computation.2 | async-start | bytes 4456448 | tf_op jit(solution)/shard_map/all_gather | solution.py:131
  8.9 223.0 %all-gather.33.cloned.1.call-start = ((), (), s32[]{:S(2)}) async-start(), calls=%async_computation.6 | async-start | bytes 37748736 | tf_op jit(solution)/shard_map/all_gather | solution.py:17
  9.9 2.5 copy-start.2
  65.3 2.8 copy-start
  75.8 254.0 %all-gather.27.cloned.1.call-start = ((), (), s32[]{:S(2)}) async-start(), calls=%async_computation.3 | async-start | bytes 4456448 | tf_op jit(solution)/shard_map/all_gather | solution.py:172
  277.7 152.3 %all-gather.29.cloned.1.call-start = ((), (), s32[]{:S(2)}) async-start(), calls=%async_computation.4 | async-start | bytes 4456448 | tf_op jit(solution)/shard_map/all_gather | solution.py:147
  329.8 6.0 copy-start.3
  379.6 330.5 %all-gather.35.cloned.1.call-start = ((), (), s32[]{:S(2)}) async-start(), calls=%async_computation.7 | async-start | bytes 37748736 | tf_op jit(solution)/shard_map/all_gather | solution.py:17
  430.1 6.1 copy-start.4
  544.8 2.2 copy-start.1
  555.9 251.9 %all-gather.31.cloned.1.call-start = ((), (), s32[]{:S(2)}) async-start(), calls=%async_computation.5 | async-start | bytes 4456448 | tf_op jit(solution)/shard_map/all_gather | solution.py:172
  807.8 6.4 copy-start.5
Sparse Core Ops, SparseCore 0:
  10.7 54.5 all-gather.24
  75.9 156.0 all-gather.32
  277.9 51.8 all-gather.26
  379.8 50.2 all-gather.28
  556.0 154.0 all-gather.34
  755.9 51.8 all-gather.30
